TPU v7x, 32 devices: a whole 2x2x4 slice. The times are simulated.
32 devices in a mesh: wide: 8 (over z, y), narrow: 4 (over x, core).
Axes of the slice: x: 2, y: 2, z: 4, core: 2. Of those that a mesh axis runs over, the one named last changes fastest.
Arguments:
- values: float32 [512, 16384], P(('wide', 'narrow')), may hold values from -200 to 200, as said below
- cloud_words: int32 [512, 512], P(('wide', 'narrow')), may hold values from -2147483648 to 2147483647, as said below
- history_len: int32 [1], replicated, may hold values from 96 to 256
- monitor_start: int32 [1], replicated, may hold values from 256 to 384
- boundary_table: int32 [512], replicated, may hold values from 500 to 2000
Outputs:
- ratio: float32 [512, 16384], P(('wide', 'narrow'))
- peak_so_far: float32 [512, 16384], P(('wide', 'narrow'))
Inputs may be any that keep to these rules, and one draw needn't show every extreme that they name: `values`: values of an index series, mixed noise and a seasonal cycle of varying scale. `cloud_words`: bit b of word j in the row of date t is 1 when pixel 32 j + b is clear at date t; the first 16 dates are clear for every pixel.
All inputs are finite; a program needn't handle non-finite values.
Results may differ from a plain program's by a relative error of at most 0.0003.
Values sent between devices are 32-bit elements; how exact they have to be, the bound alone decides.
A program may use at most 64 MiB of HBM per device.

v0:
```python
import math
import jax
import jax.numpy as jnp
from jax import lax
from jax.sharding import PartitionSpec as P

PERIOD = 46
HARMONICS = 3
COLS = 8
WINDOW = 64
HIGH = lax.Precision.HIGHEST


def unpack_clear(words):
    shifts = jnp.arange(32, dtype=jnp.int32)
    flags = jnp.bitwise_and(jnp.right_shift(words[:, :, None], shifts[None, None, :]), jnp.int32(1))
    return flags.reshape(words.shape[0], words.shape[1] * 32).astype(jnp.float32)


def harmonic_design(dates):
    day_float = jnp.arange(dates, dtype=jnp.int32).astype(jnp.float32)
    columns = [jnp.ones((dates,), jnp.float32), day_float / dates]
    for harmonic in range(1, HARMONICS + 1):
        phases = 2.0 * math.pi * harmonic / PERIOD * day_float
        columns.append(jnp.cos(phases))
        columns.append(jnp.sin(phases))
    return jnp.stack(columns, axis=1)


def solve_batched(normal_mat, target):
    size_cols = normal_mat.shape[0]
    factor = [[None] * size_cols for row_idx in range(size_cols)]
    for row_idx in range(size_cols):
        for col_idx in range(row_idx + 1):
            summed = normal_mat[row_idx, col_idx]
            for mid_idx in range(col_idx):
                summed = summed - factor[row_idx][mid_idx] * factor[col_idx][mid_idx]
            if row_idx == col_idx:
                factor[row_idx][col_idx] = jnp.sqrt(summed)
            else:
                factor[row_idx][col_idx] = summed / factor[col_idx][col_idx]
    forward = []
    for row_idx in range(size_cols):
        summed = target[row_idx]
        for mid_idx in range(row_idx):
            summed = summed - factor[row_idx][mid_idx] * forward[mid_idx]
        forward.append(summed / factor[row_idx][row_idx])
    solution = [None] * size_cols
    for row_idx in reversed(range(size_cols)):
        summed = forward[row_idx]
        for mid_idx in range(row_idx + 1, size_cols):
            summed = summed - factor[mid_idx][row_idx] * solution[mid_idx]
        solution[row_idx] = summed / factor[row_idx][row_idx]
    return jnp.stack(solution, axis=0)


def fit_statistic(values, clear, history_len, monitor_start, boundary_table):
    dates = values.shape[0]
    day = jnp.arange(dates, dtype=jnp.int32)
    design = harmonic_design(dates)
    in_history = (day < history_len[0]).astype(jnp.float32)[:, None]
    weight = clear * in_history
    outer = (design[:, :, None] * design[:, None, :]).reshape(dates, COLS * COLS)
    normal_mat = jnp.dot(
        outer.T, weight, precision=HIGH, preferred_element_type=jnp.float32
    ).reshape(COLS, COLS, -1)
    target = jnp.dot(design.T, weight * values, precision=HIGH, preferred_element_type=jnp.float32)
    coeffs = solve_batched(normal_mat, target)
    fitted = jnp.dot(design, coeffs, precision=HIGH, preferred_element_type=jnp.float32)
    resid = clear * (values - fitted)
    count = jnp.sum(weight, axis=0)
    squares = jnp.sum(weight * resid * resid, axis=0)
    sigma = jnp.sqrt(squares / (count - COLS) + 1e-06)
    lagged = day[:, None] - day[None, :]
    banded = ((lagged >= 0) & (lagged < WINDOW)).astype(jnp.float32)
    moving = jnp.dot(banded, resid, precision=HIGH, preferred_element_type=jnp.float32)
    scaled = moving / (sigma * jnp.sqrt(count))[None, :]
    bounds = boundary_table.astype(jnp.float32) * 0.001
    watching = (day >= monitor_start[0])[:, None]
    return jnp.where(watching, scaled / bounds[:, None], jnp.float32(0.0))


def per_device(values, cloud_words, history_len, monitor_start, boundary_table):
    arrived = lax.all_to_all(values, ("wide", "narrow"), split_axis=1, concat_axis=0, tiled=True)
    words = lax.all_to_all(cloud_words, ("wide", "narrow"), split_axis=1, concat_axis=0, tiled=True)
    ratio = fit_statistic(arrived, unpack_clear(words), history_len, monitor_start, boundary_table)
    rows = values.shape[0]
    blocks = ratio.reshape(ratio.shape[0] // rows, rows, ratio.shape[1])
    block_peak = lax.cummax(jnp.max(jnp.abs(blocks), axis=1), axis=0)
    earlier = jnp.concatenate([jnp.zeros_like(block_peak[:1]), block_peak[:-1]], axis=0)
    date_ratio = lax.all_to_all(ratio, ("wide", "narrow"), split_axis=0, concat_axis=1, tiled=True)
    before = lax.all_to_all(earlier, ("wide", "narrow"), split_axis=0, concat_axis=1, tiled=True)
    peak = jnp.maximum(lax.cummax(jnp.abs(date_ratio), axis=0), before)
    return (date_ratio, peak)


def solution(mesh):
    placed = (P(("wide", "narrow"), None), P(("wide", "narrow"), None), P(), P(), P())
    return jax.shard_map(
        per_device,
        mesh=mesh,
        in_specs=placed,
        out_specs=(P(("wide", "narrow"), None), P(("wide", "narrow"), None)),
        check_vma=False,
    )
```

profile of v0, /device:TPU:0, one launch (start us, length us, event | category | flops | bytes accessed | tf_op | source)
XLA Modules:
  0.0 92.7 jit_solution(12139132134094349845)
XLA Ops:
  0.6 0.0 copy-start.1
  0.6 1.0 %all_to_all.50 = s32[16,32,16]{2,1,0:T(8,128)S(1)} reshape(s32[16,512]{1,0:T(8,128)} %param.6) | data formatting | bytes 65536 | tf_op jit(solution)/shard_map/all_to_all | solution.py:85
  1.6 0.2 copy.29
  1.8 0.8 reshape.2540
  2.5 7.3 %all-to-all-start = ((s32[32,1,256]{2,1,0:T(1,128)}), s32[32,1,256]{2,1,0:T(1,128)S(1)}, u32[]{:S(2)}, u32[]{:S(2)}) async-start(s32[32,1,256]{2,1,0:T(1,128)} %reshape.2540), calls=%async_computation | async-start | bytes 65536 | tf_op jit(solution)/shard_map/all_to_all | solution.py:85
  9.9 0.1 fusion.93
  11.3 0.1 shift_right_arithmetic.38
  11.4 0.0 copy-done.1
  11.4 1.1 %copy.28 = f32[2,32,8,512]{3,2,0,1:T(8,128)} copy(f32[2,32,8,512]{3,2,1,0:T(8,128)S(1)} %bitcast.435) | data formatting | bytes 2097152 | tf_op jit(solution)/shard_map/all_to_all | solution.py:84
  12.5 0.1 fusion.91
  12.6 4.5 %all-to-all-done = s32[32,1,256]{2,1,0:T(1,128)S(1)} async-done(((s32[32,1,256]{2,1,0:T(1,128)}), s32[32,1,256]{2,1,0:T(1,128)S(1)}, u32[]{:S(2)}, u32[]{:S(2)}) %all-to-all-start) | async-done | bytes 32800 | tf_op jit(solution)/shard_map/all_to_all | solution.py:85
  17.1 2.6 %all-to-all-start.1 = ((f32[16,32,512]{2,0,1:T(8,128)}), f32[16,32,512]{2,0,1:T(8,128)S(1)}, u32[]{:S(2)}, u32[]{:S(2)}) async-start(f32[16,32,512]{2,0,1:T(8,128)} %bitcast.423), calls=%async_computation.1 | async-start | bytes 2097152 | tf_op jit(solution)/shard_map/all_to_all | solution.py:84
  19.8 0.1 fusion.95
  19.9 0.1 convert_multiply_fusion.6
  20.0 0.0 copy-start.2
  20.0 0.7 copy-done.2
  20.7 0.5 broadcast.136
  21.2 0.7 reduce.1
  21.9 0.1 reshape.2541
  22.1 0.1 copy.22
  22.2 0.1 shift_right_arithmetic.35
  22.3 0.3 copy.16
  22.6 0.3 fusion.10
  22.9 0.1 sub.3613
  23.0 0.1 sqrt.482
  23.1 1.1 %fusion.11 = f32[8,8,512]{2,1,0:T(8,128)S(1)} fusion(f32[512,512,1]{0,1,2:T(8,128)S(1)} %bitcast.432, f32[512,8]{0,1:T(8,128)S(1)} %stack.4), kind=kOutput, calls=%fused_computation.20 | convolution fusion | flops 201359360 | bytes 1196032 | tf_op jit(solution)/shard_map/dot_general | solution.py:64
  24.3 21.7 %all-to-all-done.1 = f32[16,32,512]{2,0,1:T(8,128)S(1)} async-done(((f32[16,32,512]{2,0,1:T(8,128)}), f32[16,32,512]{2,0,1:T(8,128)S(1)}, u32[]{:S(2)}, u32[]{:S(2)}) %all-to-all-start.1) | async-done | bytes 1048608 | tf_op jit(solution)/shard_map/all_to_all | solution.py:84
  46.0 0.2 bitcast_multiply_fusion
  46.2 0.6 fusion.121
  46.8 0.2 subtract_divide_fusion.6
  47.0 0.1 rsqrt_multiply_fusion
  47.1 0.2 bitcast_divide_fusion
  47.3 1.3 %fusion.2 = (f32[512]{0:T(512)S(1)}, f32[512,512]{1,0:T(8,128)S(1)}) fusion(s32[512,512]{1,0:T(8,128)S(1)} %copy.16, f32[512]{0:T(512)S(1)} %fusion.96, s32[512]{0:T(512)S(1)} %shift_right_arithmetic.38, f32[512,512]{1,0:T(8,128)S(1)} %bitcast.428, f32[512,8]{0,1:T(8,128)S(1)} %stack.4, f32[8,512]{1,0:T(8,128)S(1)} %stack.5), kind=kOutput, calls=%fused_computation.5 | convolution fusion | flops 27524608 | bytes 3184640 | tf_op jit(solution)/shard_map/dot_general | solution.py:69
  48.6 2.2 %abs_reduce_fusion = (f32[32,512]{1,0:T(8,128)S(1)}, f32[512,512]{1,0:T(8,128)}) fusion(f32[512]{0:T(512)S(1)} %convert_multiply_fusion.2, f32[512]{0:T(512)S(1)} %sqrt_multiply_fusion, f32[512,512]{1,0:T(8,128)S(1)} %get-tuple-element.85, pred[512]{0:T(512)(128)(4,1)S(1)} %iota_compare_fusion.1), kind=kOutput, calls=%fused_computation.8 | convolution fusion | flops 1612955648 | bytes 2167296 | tf_op jit(solution)/shard_map/dot_general | solution.py:76
  50.8 3.5 %all-to-all-start.2 = ((f32[32,16,512]{2,1,0:T(8,128)}), f32[32,16,512]{2,1,0:T(8,128)S(1)}, u32[]{:S(2)}, u32[]{:S(2)}) async-start(f32[32,16,512]{2,1,0:T(8,128)} %bitcast.50), calls=%async_computation.2 | async-start | bytes 2097152 | tf_op jit(solution)/shard_map/all_to_all | solution.py:91
  54.4 0.1 reduce_window_max.21
  54.5 0.7 copy.20
  55.2 25.4 %all-to-all-done.2 = f32[32,16,512]{2,1,0:T(8,128)S(1)} async-done(((f32[32,16,512]{2,1,0:T(8,128)}), f32[32,16,512]{2,1,0:T(8,128)S(1)}, u32[]{:S(2)}, u32[]{:S(2)}) %all-to-all-start.2) | async-done | bytes 1048608 | tf_op jit(solution)/shard_map/all_to_all | solution.py:91
  80.6 3.6 %all-to-all-start.3 = ((f32[32,1,512]{2,1,0:T(1,128)}), f32[32,1,512]{2,1,0:T(1,128)S(1)}, u32[]{:S(2)}, u32[]{:S(2)}) async-start(f32[32,1,512]{2,1,0:T(1,128)} %copy.20), calls=%async_computation.3 | async-start | bytes 131072 | tf_op jit(solution)/shard_map/all_to_all | solution.py:92
  84.2 0.1 copy.25
  84.3 0.0 copy-start
  84.3 0.1 abs.6
  84.4 0.9 copy-done
  85.3 0.9 reduce_window_max.20
  86.2 5.4 %all-to-all-done.3 = f32[32,1,512]{2,1,0:T(1,128)S(1)} async-done(((f32[32,1,512]{2,1,0:T(1,128)}), f32[32,1,512]{2,1,0:T(1,128)S(1)}, u32[]{:S(2)}, u32[]{:S(2)}) %all-to-all-start.3) | async-done | bytes 65568 | tf_op jit(solution)/shard_map/all_to_all | solution.py:92
  91.6 1.1 %broadcast_maximum_fusion = f32[16,16384]{1,0:T(8,128)} fusion(f32[16,16384]{1,0:T(8,128)S(1)} %reduce_window_max.20, f32[16384]{0:T(1024)S(1)} %bitcast.437), kind=kLoop, calls=%fused_computation.16 | loop fusion | flops 262144 | bytes 2162688 | tf_op jit(solution)/shard_map/max | solution.py:93
  (13 shorter events, 0.2 us)
Async XLA Ops:
  0.6 10.8 %copy-start.1 = (f32[16,16384]{1,0:T(8,128)S(1)}, f32[16,16384]{1,0:T(8,128)}, u32[]{:S(2)}) copy-start(f32[16,16384]{1,0:T(8,128)} %param.5) | copy-start | bytes 3145732
  2.5 14.6 %all-to-all-start = ((s32[32,1,256]{2,1,0:T(1,128)}), s32[32,1,256]{2,1,0:T(1,128)S(1)}, u32[]{:S(2)}, u32[]{:S(2)}) async-start(s32[32,1,256]{2,1,0:T(1,128)} %reshape.2540), calls=%async_computation | async-start | bytes 65536 | tf_op jit(solution)/shard_map/all_to_all | solution.py:85
  17.1 28.8 %all-to-all-start.1 = ((f32[16,32,512]{2,0,1:T(8,128)}), f32[16,32,512]{2,0,1:T(8,128)S(1)}, u32[]{:S(2)}, u32[]{:S(2)}) async-start(f32[16,32,512]{2,0,1:T(8,128)} %bitcast.423), calls=%async_computation.1 | async-start | bytes 2097152 | tf_op jit(solution)/shard_map/all_to_all | solution.py:84
  20.0 0.7 copy-start.2
  50.8 29.8 %all-to-all-start.2 = ((f32[32,16,512]{2,1,0:T(8,128)}), f32[32,16,512]{2,1,0:T(8,128)S(1)}, u32[]{:S(2)}, u32[]{:S(2)}) async-start(f32[32,16,512]{2,1,0:T(8,128)} %bitcast.50), calls=%async_computation.2 | async-start | bytes 2097152 | tf_op jit(solution)/shard_map/all_to_all | solution.py:91
  80.6 11.0 %all-to-all-start.3 = ((f32[32,1,512]{2,1,0:T(1,128)}), f32[32,1,512]{2,1,0:T(1,128)S(1)}, u32[]{:S(2)}, u32[]{:S(2)}) async-start(f32[32,1,512]{2,1,0:T(1,128)} %copy.20), calls=%async_computation.3 | async-start | bytes 131072 | tf_op jit(solution)/shard_map/all_to_all | solution.py:92
  84.3 1.0 %copy-start = (f32[32,2,8,512]{3,2,0,1:T(8,128)}, f32[32,2,8,512]{3,2,0,1:T(8,128)S(1)}, u32[]{:S(2)}) copy-start(f32[32,2,8,512]{3,2,0,1:T(8,128)S(1)} %copy.25) | copy-start | bytes 3145732
where the time goes:
time: 93.1 us; the launch traced here: 92.7 us
  waiting for transfers between devices  57 us (61%)
  starting transfers between devices  17.1 us (18%)
  local copies, waits for them, and re-layouts  6.78 us (7%)
  matrix products  5.22 us (6%)
  other arithmetic  4.33 us (5%)
  between operations  2.16 us (2%)
    all_to_all x1, waiting for transfers between devices, per_device(): lax.all_to_all(ratio, ('wide', 'narrow'), split_axis=0, concat_axis=1, ti...  25.4 us
    all_to_all x1, waiting for transfers between devices, per_device(): lax.all_to_all(values, ('wide', 'narrow'), split_axis=1, concat_axis=0, t...  21.7 us
    all_to_all x1, starting transfers between devices, per_device(): lax.all_to_all(cloud_words, ('wide', 'narrow'), split_axis=1, concat_axis...  7.33 us
    all_to_all x1, waiting for transfers between devices, per_device(): lax.all_to_all(earlier, ('wide', 'narrow'), split_axis=0, concat_axis=1,...  5.43 us
    all_to_all x1, waiting for transfers between devices, per_device(): lax.all_to_all(cloud_words, ('wide', 'narrow'), split_axis=1, concat_axis...  4.54 us
    all_to_all x1, starting transfers between devices, per_device(): lax.all_to_all(earlier, ('wide', 'narrow'), split_axis=0, concat_axis=1,...  3.62 us
    all_to_all x1, starting transfers between devices, per_device(): lax.all_to_all(ratio, ('wide', 'narrow'), split_axis=0, concat_axis=1, ti...  3.54 us
    all_to_all x1, starting transfers between devices, per_device(): lax.all_to_all(values, ('wide', 'narrow'), split_axis=1, concat_axis=0, t...  2.65 us
  transfers between devices with their start and end apart: 4, of which 4 were waited for; matrix products, arithmetic and copies ran while one was open for 8% of the time, Pallas kernels for 0%

commit v1 on v0

--- a/solution.py
+++ b/solution.py
@@ -81,7 +81,13 @@
 
 
 def per_device(values, cloud_words, history_len, monitor_start, boundary_table):
-    arrived = lax.all_to_all(values, ("wide", "narrow"), split_axis=1, concat_axis=0, tiled=True)
+    compute_the_shards = lambda my_data, comm_axis: jnp.concatenate(
+        lax.all_to_all(
+            jnp.stack(jnp.split(my_data, lax.axis_size(comm_axis), 1), 0), comm_axis, 0, 0
+        ),
+        0,
+    )
+    arrived = compute_the_shards(values, ("wide", "narrow"))
     words = lax.all_to_all(cloud_words, ("wide", "narrow"), split_axis=1, concat_axis=0, tiled=True)
     ratio = fit_statistic(arrived, unpack_clear(words), history_len, monitor_start, boundary_table)
     rows = values.shape[0]

time: 93.1 us -> 111 us (1.19)
  local copies, waits for them, and re-layouts: 6.78 us -> 25.5 us
  waiting for transfers between devices: 57 us -> 52.5 us
  starting transfers between devices: 17.1 us -> 20.4 us
    unnamed x8 -> x39, local copies, waits for them, and re-layouts: 2.42 us -> 21.5 us
    all_to_all x1, waiting for transfers between devices: 4.54 us -> 0.01 us  [per_device(): lax.all_to_all(cloud_words, ('wide', 'narrow'), split_axis=1, concat_axis...]
    all_to_all x1, starting transfers between devices: 2.65 us -> 5.84 us  [per_device(): lax.all_to_all(jnp.stack(jnp.split(my_data, lax.axis_size(comm_axis), 1),...]
  transfers between devices with their start and end apart: 4 -> 4, of which waited for: 4 -> 3; matrix products, arithmetic and copies ran while one was open for 8% -> 23% of each run, Pallas kernels for 0% -> 0%
where the time goes in v1:
time: 111 us; the launch traced here: 110 us
  waiting for transfers between devices  52.5 us (47%)
  local copies, waits for them, and re-layouts  25.5 us (23%)
  starting transfers between devices  20.4 us (18%)
  matrix products  5.22 us (5%)
  other arithmetic  4.33 us (4%)
  between operations  2.19 us (2%)
    all_to_all x1, waiting for transfers between devices, per_device(): lax.all_to_all(ratio, ('wide', 'narrow'), split_axis=0, concat_axis=1, ti...  25.4 us
    all_to_all x1, waiting for transfers between devices, per_device(): lax.all_to_all(jnp.stack(jnp.split(my_data, lax.axis_size(comm_axis), 1),...  21.7 us
    unnamed x39, local copies, waits for them, and re-layouts  21.5 us
    all_to_all x1, starting transfers between devices, per_device(): lax.all_to_all(cloud_words, ('wide', 'narrow'), split_axis=1, concat_axis...  7.33 us
    all_to_all x1, starting transfers between devices, per_device(): lax.all_to_all(jnp.stack(jnp.split(my_data, lax.axis_size(comm_axis), 1),...  5.84 us
    all_to_all x1, waiting for transfers between devices, per_device(): lax.all_to_all(earlier, ('wide', 'narrow'), split_axis=0, concat_axis=1,...  5.43 us
    all_to_all x1, starting transfers between devices, per_device(): lax.all_to_all(ratio, ('wide', 'narrow'), split_axis=0, concat_axis=1, ti...  3.62 us
    all_to_all x1, starting transfers between devices, per_device(): lax.all_to_all(earlier, ('wide', 'narrow'), split_axis=0, concat_axis=1,...  3.62 us
  transfers between devices with their start and end apart: 4, of which 3 were waited for; matrix products, arithmetic and copies ran while one was open for 23% of the time, Pallas kernels for 0%

profile of v1, /device:TPU:0, one launch (start us, length us, event | category | flops | bytes accessed | tf_op | source)
XLA Modules:
  0.0 110.1 jit_solution(10329535436238484293)
XLA Ops:
  0.6 1.0 all_to_all.39
  1.8 0.8 reshape.2541
  2.5 7.3 %all-to-all-start = ((s32[32,1,256]{2,1,0:T(1,128)}), s32[32,1,256]{2,1,0:T(1,128)S(1)}, u32[]{:S(2)}, u32[]{:S(2)}) async-start(s32[32,1,256]{2,1,0:T(1,128)} %reshape.2541), calls=%async_computation | async-start | bytes 65536 | tf_op jit(solution)/shard_map/all_to_all | solution.py:91
  11.4 0.6 constant_dynamic-update-slice_fusion.31
  12.0 0.6 constant_dynamic-update-slice_fusion.30
  12.6 0.6 constant_dynamic-update-slice_fusion.29
  13.2 0.6 constant_dynamic-update-slice_fusion.28
  13.9 0.6 constant_dynamic-update-slice_fusion.27
  14.5 0.6 constant_dynamic-update-slice_fusion.26
  15.1 0.6 constant_dynamic-update-slice_fusion.25
  15.7 0.6 constant_dynamic-update-slice_fusion.24
  16.3 0.6 constant_dynamic-update-slice_fusion.23
  17.0 0.6 constant_dynamic-update-slice_fusion.22
  17.6 0.6 constant_dynamic-update-slice_fusion.21
  18.2 0.6 constant_dynamic-update-slice_fusion.20
  18.8 0.6 constant_dynamic-update-slice_fusion.19
  19.4 0.6 constant_dynamic-update-slice_fusion.18
  20.0 0.6 constant_dynamic-update-slice_fusion.17
  20.7 0.6 constant_dynamic-update-slice_fusion.16
  21.3 0.6 constant_dynamic-update-slice_fusion.15
  21.9 0.6 constant_dynamic-update-slice_fusion.14
  22.5 0.6 constant_dynamic-update-slice_fusion.13
  23.1 0.6 constant_dynamic-update-slice_fusion.12
  23.7 0.6 constant_dynamic-update-slice_fusion.11
  24.4 0.6 constant_dynamic-update-slice_fusion.10
  25.0 0.6 constant_dynamic-update-slice_fusion.9
  25.6 0.6 constant_dynamic-update-slice_fusion.8
  26.2 0.6 constant_dynamic-update-slice_fusion.7
  26.8 0.6 constant_dynamic-update-slice_fusion.6
  27.4 0.6 constant_dynamic-update-slice_fusion.5
  28.1 0.6 constant_dynamic-update-slice_fusion.4
  28.7 0.6 constant_dynamic-update-slice_fusion.3
  29.3 0.6 constant_dynamic-update-slice_fusion.2
  31.3 5.8 %all-to-all-start.1 = ((f32[32,16,512]{2,1,0:T(8,128)}), f32[32,16,512]{2,1,0:T(8,128)S(1)}, u32[]{:S(2)}, u32[]{:S(2)}) async-start(f32[32,16,512]{2,1,0:T(8,128)} %constant_dynamic-update-slice_fusion), calls=%async_computation.1 | async-start | bytes 2097152 | tf_op jit(solution)/shard_map/all_to_all | solution.py:85
  37.4 0.7 copy-done.2
  38.6 0.7 reduce.1
  40.4 1.1 %fusion.11 = f32[8,8,512]{2,1,0:T(8,128)S(1)} fusion(f32[512,512,1]{0,1,2:T(8,128)S(1)} %bitcast.490, f32[512,8]{0,1:T(8,128)S(1)} %stack.153), kind=kOutput, calls=%fused_computation.19 | convolution fusion | flops 201359360 | bytes 1196032 | tf_op jit(solution)/shard_map/dot_general | solution.py:64
  41.7 21.7 %all-to-all-done.1 = f32[32,16,512]{2,1,0:T(8,128)S(1)} async-done(((f32[32,16,512]{2,1,0:T(8,128)}), f32[32,16,512]{2,1,0:T(8,128)S(1)}, u32[]{:S(2)}, u32[]{:S(2)}) %all-to-all-start.1) | async-done | bytes 1048608 | tf_op jit(solution)/shard_map/all_to_all | solution.py:85
  64.7 1.3 %fusion.2 = (f32[512]{0:T(512)S(1)}, f32[512,512]{1,0:T(8,128)S(1)}) fusion(s32[512,512]{1,0:T(8,128)S(1)} %copy.14, f32[512]{0:T(512)S(1)} %fusion.96, s32[512]{0:T(512)S(1)} %shift_right_arithmetic.38, f32[512,512]{1,0:T(8,128)S(1)} %bitcast.486, f32[512,8]{0,1:T(8,128)S(1)} %stack.153, f32[8,512]{1,0:T(8,128)S(1)} %stack.154), kind=kOutput, calls=%fused_computation.5 | convolution fusion | flops 27524608 | bytes 3184640 | tf_op jit(solution)/shard_map/dot_general | solution.py:69
  66.0 2.2 %abs_reduce_fusion = (f32[32,512]{1,0:T(8,128)S(1)}, f32[512,512]{1,0:T(8,128)}) fusion(f32[512]{0:T(512)S(1)} %convert_multiply_fusion.2, f32[512]{0:T(512)S(1)} %sqrt_multiply_fusion, f32[512,512]{1,0:T(8,128)S(1)} %get-tuple-element.85, pred[512]{0:T(512)(128)(4,1)S(1)} %iota_compare_fusion.1), kind=kOutput, calls=%fused_computation.7 | convolution fusion | flops 1612955648 | bytes 2167296 | tf_op jit(solution)/shard_map/dot_general | solution.py:76
  68.2 3.6 %all-to-all-start.2 = ((f32[32,16,512]{2,1,0:T(8,128)}), f32[32,16,512]{2,1,0:T(8,128)S(1)}, u32[]{:S(2)}, u32[]{:S(2)}) async-start(f32[32,16,512]{2,1,0:T(8,128)} %bitcast.80), calls=%async_computation.2 | async-start | bytes 2097152 | tf_op jit(solution)/shard_map/all_to_all | solution.py:97
  71.9 0.7 copy.17
  72.6 25.4 %all-to-all-done.2 = f32[32,16,512]{2,1,0:T(8,128)S(1)} async-done(((f32[32,16,512]{2,1,0:T(8,128)}), f32[32,16,512]{2,1,0:T(8,128)S(1)}, u32[]{:S(2)}, u32[]{:S(2)}) %all-to-all-start.2) | async-done | bytes 1048608 | tf_op jit(solution)/shard_map/all_to_all | solution.py:97
  98.0 3.6 %all-to-all-start.3 = ((f32[32,1,512]{2,1,0:T(1,128)}), f32[32,1,512]{2,1,0:T(1,128)S(1)}, u32[]{:S(2)}, u32[]{:S(2)}) async-start(f32[32,1,512]{2,1,0:T(1,128)} %copy.17), calls=%async_computation.3 | async-start | bytes 131072 | tf_op jit(solution)/shard_map/all_to_all | solution.py:98
  101.8 0.9 copy-done
  102.7 0.9 reduce_window_max.20
  103.6 5.4 %all-to-all-done.3 = f32[32,1,512]{2,1,0:T(1,128)S(1)} async-done(((f32[32,1,512]{2,1,0:T(1,128)}), f32[32,1,512]{2,1,0:T(1,128)S(1)}, u32[]{:S(2)}, u32[]{:S(2)}) %all-to-all-start.3) | async-done | bytes 65568 | tf_op jit(solution)/shard_map/all_to_all | solution.py:98
  109.1 1.1 broadcast_maximum_fusion
  (42 shorter events, 5.2 us)
Async XLA Ops:
  0.6 10.8 %copy-start.1 = (f32[16,16384]{1,0:T(8,128)S(1)}, f32[16,16384]{1,0:T(8,128)}, u32[]{:S(2)}) copy-start(f32[16,16384]{1,0:T(8,128)} %param.5) | copy-start | bytes 3145732
  2.5 28.7 %all-to-all-start = ((s32[32,1,256]{2,1,0:T(1,128)}), s32[32,1,256]{2,1,0:T(1,128)S(1)}, u32[]{:S(2)}, u32[]{:S(2)}) async-start(s32[32,1,256]{2,1,0:T(1,128)} %reshape.2541), calls=%async_computation | async-start | bytes 65536 | tf_op jit(solution)/shard_map/all_to_all | solution.py:91
  31.3 32.1 %all-to-all-start.1 = ((f32[32,16,512]{2,1,0:T(8,128)}), f32[32,16,512]{2,1,0:T(8,128)S(1)}, u32[]{:S(2)}, u32[]{:S(2)}) async-start(f32[32,16,512]{2,1,0:T(8,128)} %constant_dynamic-update-slice_fusion), calls=%async_computation.1 | async-start | bytes 2097152 | tf_op jit(solution)/shard_map/all_to_all | solution.py:85
  37.4 0.7 copy-start.2
  68.2 29.8 %all-to-all-start.2 = ((f32[32,16,512]{2,1,0:T(8,128)}), f32[32,16,512]{2,1,0:T(8,128)S(1)}, u32[]{:S(2)}, u32[]{:S(2)}) async-start(f32[32,16,512]{2,1,0:T(8,128)} %bitcast.80), calls=%async_computation.2 | async-start | bytes 2097152 | tf_op jit(solution)/shard_map/all_to_all | solution.py:97
  98.0 11.0 %all-to-all-start.3 = ((f32[32,1,512]{2,1,0:T(1,128)}), f32[32,1,512]{2,1,0:T(1,128)S(1)}, u32[]{:S(2)}, u32[]{:S(2)}) async-start(f32[32,1,512]{2,1,0:T(1,128)} %copy.17), calls=%async_computation.3 | async-start | bytes 131072 | tf_op jit(solution)/shard_map/all_to_all | solution.py:98
  101.7 1.0 copy-start
